TPU v7x, 32 devices: a whole 2x2x4 slice. The times are simulated.
32 devices in a mesh: scan: 8 (over y, x, core), grp: 4 (over z).
Axes of the slice: x: 2, y: 2, z: 4, core: 2. Of those that a mesh axis runs over, the one named last changes fastest.
Arguments:
- frames: bfloat16 [256, 1024, 1024], P('scan', 'grp'), may hold values from -6 to 6
- dark_frame: int32 [36864], replicated, may hold values from 0 to 15
- gain_frame: int32 [36864], replicated, may hold values from 3072 to 5120
- bf_index: int32 [1024], replicated, may hold values from 0 to 36863
- row_level: float32 [256], P('scan'), may hold values from 0.5 to 2
- shift_num: int32 [2, 1024], P(None, ('scan', 'grp')), may hold values from -32 to 32
Outputs:
- upsampled: float32 [512, 2048], P(('scan', 'grp'))
- correlation: float32 [1024, 256], P(('scan', 'grp'))
All inputs are finite; a program needn't handle non-finite values.
Results may differ from a plain program's by a relative error of at most 0.0085.
Values may be sent and summed in bfloat16 or wider, within the bound.
A program may use at most 128 MiB of HBM per device.

v0:
```python
import math

import jax
import jax.numpy as jnp
from jax import lax
from jax.sharding import PartitionSpec as P

BF = 1024
LAGS = 16
DEN = 4


def signed_freq(length):
    indices = jnp.arange(length, dtype=jnp.int32)
    return jnp.where(indices < length // 2, indices, indices - length)


def phase_pair(leading, trailing, period):
    product = jnp.mod(leading[:, None] * trailing[None, :], period)
    angles = product.astype(jnp.float32) * (2.0 * math.pi / period)
    return (jnp.cos(angles), jnp.sin(angles))


def low_dot(left, right):
    return jnp.dot(left, right, preferred_element_type=jnp.float32)


def exact_dot(left, right):
    return jnp.dot(left, right, precision=lax.Precision.HIGHEST, preferred_element_type=jnp.float32)


def split_dot(table, values):
    upper = values.astype(jnp.bfloat16)
    lower = (values - upper.astype(jnp.float32)).astype(jnp.bfloat16)
    return low_dot(table, upper) + low_dot(table, lower)


def forward_pair(picture, cosine_cols, sine_cols, cosine_rows, sine_rows):
    real_rows = low_dot(picture, cosine_cols).astype(jnp.bfloat16)
    imag_rows = (-low_dot(picture, sine_cols)).astype(jnp.bfloat16)
    real_part = low_dot(cosine_rows, real_rows) + low_dot(sine_rows, imag_rows)
    imag_part = low_dot(cosine_rows, imag_rows) - low_dot(sine_rows, real_rows)
    anchor = (jnp.arange(real_part.shape[0])[:, None] == 0) & (
        jnp.arange(real_part.shape[1])[None, :] == 0
    )
    return (jnp.where(anchor, 0.0, real_part), jnp.where(anchor, 0.0, imag_part))


def axis_phase(length, amount):
    product = jnp.mod(signed_freq(length) * amount, DEN * length)
    angles = product.astype(jnp.float32) * (2.0 * math.pi / (DEN * length))
    return (jnp.cos(angles), jnp.sin(angles))


def shift_apply(real_part, imag_part, amounts):
    cosine_y, sine_y = axis_phase(real_part.shape[0], amounts[0])
    cosine_x, sine_x = axis_phase(real_part.shape[1], amounts[1])
    cos_phi = cosine_y[:, None] * cosine_x[None, :] - sine_y[:, None] * sine_x[None, :]
    sin_phi = sine_y[:, None] * cosine_x[None, :] + cosine_y[:, None] * sine_x[None, :]
    real_shift = (real_part * cos_phi + imag_part * sin_phi).astype(jnp.bfloat16)
    imag_shift = (imag_part * cos_phi - real_part * sin_phi).astype(jnp.bfloat16)
    return (real_shift, imag_shift)


def correlate(real_part, imag_part, ref_real, ref_imag, lag_tables, scale):
    lag_rows_cos, lag_rows_sin, lag_cols_cos, lag_cols_sin = lag_tables
    cross_real = (real_part * ref_real + imag_part * ref_imag).astype(jnp.bfloat16)
    cross_imag = (imag_part * ref_real - real_part * ref_imag).astype(jnp.bfloat16)
    half_real = low_dot(lag_rows_cos, cross_real) - low_dot(lag_rows_sin, cross_imag)
    half_imag = low_dot(lag_rows_cos, cross_imag) + low_dot(lag_rows_sin, cross_real)
    return (
        (exact_dot(half_real, lag_cols_cos) - exact_dot(half_imag, lag_cols_sin)) * scale
    ).reshape(-1)


def local(frames, dark_frame, gain_frame, bf_index, row_level, shift_num):
    dark_pixel = jnp.take(dark_frame, bf_index).astype(jnp.float32) / 256.0
    gain_pixel = jnp.take(gain_frame, bf_index).astype(jnp.float32) / 4096.0
    corrected = (frames.astype(jnp.float32) - row_level[:, None, None] * dark_pixel) * gain_pixel
    ref_local = jnp.sum(corrected, axis=2).astype(jnp.bfloat16)
    strips = jnp.transpose(corrected, (2, 0, 1)).astype(jnp.bfloat16)
    ref_strip = lax.all_gather(ref_local, "grp", axis=1, tiled=True)
    ref_image = lax.all_gather(ref_strip, "scan", axis=0, tiled=True)
    mixed = lax.all_to_all(strips, ("scan", "grp"), split_axis=0, concat_axis=1, tiled=True)
    scan_count = lax.axis_size("scan")
    grp_count = lax.axis_size("grp")
    owned = mixed.shape[0]
    strip_rows = strips.shape[1]
    strip_cols = strips.shape[2]
    pictures = mixed.reshape(owned, scan_count, grp_count, strip_rows, strip_cols)
    pictures = pictures.transpose(0, 1, 3, 2, 4).reshape(
        owned, scan_count * strip_rows, grp_count * strip_cols
    )
    rows = pictures.shape[1]
    cols = pictures.shape[2]
    row_range = jnp.arange(rows, dtype=jnp.int32)
    col_range = jnp.arange(cols, dtype=jnp.int32)
    cosine_cols, sine_cols = phase_pair(col_range, col_range, cols)
    cosine_rows, sine_rows = phase_pair(row_range, row_range, rows)
    tables = (
        cosine_cols.astype(jnp.bfloat16),
        sine_cols.astype(jnp.bfloat16),
        cosine_rows.astype(jnp.bfloat16),
        sine_rows.astype(jnp.bfloat16),
    )
    up_rows_cos, up_rows_sin = phase_pair(
        jnp.arange(2 * rows, dtype=jnp.int32), signed_freq(rows), 2 * rows
    )
    up_rows_cos = up_rows_cos.astype(jnp.bfloat16)
    up_rows_sin = up_rows_sin.astype(jnp.bfloat16)
    up_cols_cos, up_cols_sin = phase_pair(
        signed_freq(cols), jnp.arange(2 * cols, dtype=jnp.int32), 2 * cols
    )
    up_cols_cos = up_cols_cos.astype(jnp.bfloat16)
    up_cols_sin = up_cols_sin.astype(jnp.bfloat16)
    lag_values = jnp.arange(LAGS, dtype=jnp.int32) - LAGS // 2
    lag_rows_cos, lag_rows_sin = phase_pair(lag_values, row_range, rows)
    lag_rows_cos = lag_rows_cos.astype(jnp.bfloat16)
    lag_rows_sin = lag_rows_sin.astype(jnp.bfloat16)
    lag_cols_cos, lag_cols_sin = phase_pair(col_range, lag_values, cols)
    lag_tables = (lag_rows_cos, lag_rows_sin, lag_cols_cos, lag_cols_sin)
    corr_scale = 1.0 / (rows * cols * math.sqrt(BF * rows * cols))
    ref_real, ref_imag = forward_pair(ref_image, *tables)

    def accumulate(totals, real_shift, imag_shift):
        return (
            totals[0] + real_shift.astype(jnp.float32),
            totals[1] + imag_shift.astype(jnp.float32),
        )

    start_totals = (jnp.zeros((rows, cols), jnp.float32), jnp.zeros((rows, cols), jnp.float32))

    def visit(totals, element):
        picture, amounts = element
        real_part, imag_part = forward_pair(picture, *tables)
        correl = correlate(real_part, imag_part, ref_real, ref_imag, lag_tables, corr_scale)
        real_shift, imag_shift = shift_apply(real_part, imag_part, amounts)
        return (accumulate(totals, real_shift, imag_shift), correl)

    totals, correls = lax.scan(visit, start_totals, (pictures, shift_num.T))
    part_real, part_imag = (
        lax.psum_scatter(totals[0], ("scan", "grp"), scatter_dimension=1, tiled=True),
        lax.psum_scatter(totals[1], ("scan", "grp"), scatter_dimension=1, tiled=True),
    )
    column_real = split_dot(up_rows_cos, part_real) - split_dot(up_rows_sin, part_imag)
    column_imag = split_dot(up_rows_cos, part_imag) + split_dot(up_rows_sin, part_real)
    rows_real, rows_imag = (
        lax.all_to_all(
            column_real.astype(jnp.bfloat16),
            ("scan", "grp"),
            split_axis=0,
            concat_axis=1,
            tiled=True,
        ),
        lax.all_to_all(
            column_imag.astype(jnp.bfloat16),
            ("scan", "grp"),
            split_axis=0,
            concat_axis=1,
            tiled=True,
        ),
    )
    upsampled = (low_dot(rows_real, up_cols_cos) - low_dot(rows_imag, up_cols_sin)) * (
        1.0 / (rows * cols * math.sqrt(BF))
    )
    return (upsampled, correls)


def solution(mesh):
    return jax.shard_map(
        local,
        mesh=mesh,
        in_specs=(P("scan", "grp", None), P(), P(), P(), P("scan"), P(None, ("scan", "grp"))),
        out_specs=(P(("scan", "grp"), None), P(("scan", "grp"), None)),
        check_vma=False,
    )
```

profile of v0, /device:TPU:0, one launch (start us, length us, event | category | flops | bytes accessed | tf_op | source)
XLA Modules:
  0.0 2638.5 jit_solution(18040160947893467107)
XLA Ops:
  20.4 23.9 copy.18
  44.6 17.6 fusion.125
  69.8 378.6 %all_gather.6 = bf16[32,1024]{1,0:T(8,128)(2,1)S(1)} all-gather(bf16[32,256]{1,0:T(8,128)(2,1)S(1)} %get-tuple-element.481), channel_id=1, replica_groups=mesh['scan'=8,'grp'=4] {'grp'}, dimensions={1}, use_global_device_ids=true | all-gather | bytes 81920 | tf_op jit(solution)/shard_map/all_gather | solution.py:82
  501.8 20.0 copy.20
  521.8 27.4 %reshape.144 = bf16[32,256,1024]{2,1,0:T(8,128)(2,1)} reshape(bf16[32,8,32,4,256]{4,3,2,1,0:T(4,128)(2,1)} %copy.20) | data formatting | bytes 33554432 | tf_op jit(solution)/shard_map/reshape | solution.py:91
  549.2 1714.4 %while.21 = (s32[]{:T(128)}, f32[256,1024]{0,1:T(8,128)S(1)}, f32[256,1024]{0,1:T(8,128)}, f32[32,256]{1,0:T(8,128)S(1)}, bf16[32,256,1024]{2,1,0:T(8,128)(2,1)}...) while((s32[]{:T(128)}, f32[256,1024]{0,1:T(8,128)S(1)}, ...), condition=%wide.region_2.4_spmd.clone.clone.clone.clone, body=%wide.region_1.3_spmd.clone.clone.clone.clone.sunk | while | flops 1696308224 | bytes 22577476 | solution.py:140
  549.7 17.4 fusion.307
  568.3 17.2 fusion.309
  602.9 17.3 fusion.307
  621.5 17.2 fusion.309
  656.5 17.4 fusion.307
  710.1 17.4 fusion.307
  763.6 17.4 fusion.307
  817.2 17.4 fusion.307
  870.8 17.4 fusion.307
  889.4 17.2 fusion.309
  924.3 17.4 fusion.307
  977.9 17.4 fusion.307
  1031.5 17.4 fusion.307
  1085.0 17.4 fusion.307
  1138.6 17.4 fusion.307
  1157.2 17.2 fusion.309
  1192.2 17.4 fusion.307
  1245.7 17.4 fusion.307
  1299.3 17.4 fusion.307
  1352.9 17.4 fusion.307
  1406.4 17.4 fusion.307
  1460.0 17.4 fusion.307
  1513.6 17.4 fusion.307
  1567.1 17.4 fusion.307
  1620.7 17.4 fusion.307
  1674.3 17.4 fusion.307
  1727.8 17.4 fusion.307
  1781.4 17.4 fusion.307
  1835.0 17.4 fusion.307
  1888.5 17.4 fusion.307
  1907.1 17.2 fusion.309
  1942.1 17.4 fusion.307
  1995.7 17.4 fusion.307
  2049.2 17.4 fusion.307
  2102.8 17.4 fusion.307
  2156.4 17.4 fusion.307
  2175.0 17.2 fusion.309
  2209.9 17.4 fusion.307
  2265.4 134.1 %reduce-scatter.3.cloned.1.call-done = f32[256,32]{0,1:T(8,128)} async-done(((f32[256,1024]{0,1:T(8,128)}), f32[256,32]{0,1:T(8,128)}) %reduce-scatter.3.cloned.1.call-update) | async-done | bytes 32784 | tf_op jit(solution)/shard_map/reduce_scatter | solution.py:142
  2405.2 130.1 %reduce-scatter.5.cloned.1.call-done = f32[256,32]{0,1:T(8,128)} async-done(((f32[256,1024]{0,1:T(8,128)}), f32[256,32]{0,1:T(8,128)}) %reduce-scatter.5.cloned.1.call-update) | async-done | bytes 32784 | tf_op jit(solution)/shard_map/reduce_scatter | solution.py:143
  2567.7 31.2 %fusion.137 = f32[16,2048]{1,0:T(8,128)S(1)} fusion(bf16[16,1024]{1,0:T(8,128)(2,1)S(1)} %all_to_all.45, s32[1024]{0:T(1024)S(1)} %compare_select_fusion.5), kind=kOutput, calls=%fused_computation.178 | convolution fusion | flops 98566144 | bytes 167936 | tf_op jit(solution)/shard_map/dot_general | solution.py:25
  2598.9 32.5 %fusion.145 = f32[16,2048]{1,0:T(8,128)} fusion(f32[16,2048]{1,0:T(8,128)S(1)} %fusion.137, bf16[16,1024]{1,0:T(8,128)(2,1)S(1)} %all_to_all.49, s32[1024]{0:T(1024)S(1)} %compare_select_fusion.5), kind=kOutput, calls=%fused_computation.186 | convolution fusion | flops 98631680 | bytes 299008 | tf_op jit(solution)/shard_map/dot_general | solution.py:25
  (741 shorter events, 1166.4 us)
Async XLA Ops:
  7.2 0.9 copy-start
  7.2 7.1 copy-start.8
  7.2 7.1 copy-start.2
  20.4 23.9 copy-start.9
  62.2 439.6 %all-to-all-start = ((bf16[1024,32,256]{2,1,0:T(8,128)(2,1)}), bf16[1024,32,256]{2,1,0:T(8,128)(2,1)}, u32[]{:S(2)}, u32[]{:S(2)}) async-start(bf16[1024,32,256]{2,1,0:T(8,128)(2,1)} %get-tuple-element.482), calls=%async_computation | async-start | bytes 33554432 | tf_op jit(solution)/shard_map/all_to_all | solution.py:84
  69.7 2329.8 %reduce-scatter.3.cloned.1.call-start = ((), (), s32[]{:S(2)}) async-start(), calls=%async_computation.5 | async-start | bytes 1081344 | tf_op jit(solution)/shard_map/reduce_scatter | solution.py:142
  474.7 17.7 copy-start.5
  521.8 27.4 %copy-start.7 = (s32[2,32]{1,0:T(2,128)S(1)}, s32[2,32]{1,0:T(2,128)}, u32[]{:S(2)}) copy-start(s32[2,32]{1,0:T(2,128)} %param.15) | copy-start | bytes 772
  567.0 18.5 copy-start.4
  620.3 18.5 copy-start.4
  673.9 18.5 copy-start.4
  727.4 18.5 copy-start.4
  781.0 18.5 copy-start.4
  834.6 18.5 copy-start.4
  888.1 18.5 copy-start.4
  941.7 18.5 copy-start.4
  995.3 18.5 copy-start.4
  1048.8 18.5 copy-start.4
  1102.4 18.5 copy-start.4
  1156.0 18.5 copy-start.4
  1209.5 18.5 copy-start.4
  1263.1 18.5 copy-start.4
  1316.7 18.5 copy-start.4
  1370.2 18.5 copy-start.4
  1423.8 18.5 copy-start.4
  1477.3 18.5 copy-start.4
  1530.9 18.5 copy-start.4
  1584.5 18.5 copy-start.4
  1638.0 18.5 copy-start.4
  1691.6 18.5 copy-start.4
  1745.2 18.5 copy-start.4
  1798.7 18.5 copy-start.4
  1852.3 18.5 copy-start.4
  1905.9 18.5 copy-start.4
  1959.4 18.5 copy-start.4
  2013.0 18.5 copy-start.4
  2066.6 18.5 copy-start.4
  2120.1 18.5 copy-start.4
  2173.7 18.5 copy-start.4
  2227.3 18.5 copy-start.4
  2263.7 1.0 copy-start.3
  2263.7 274.6 %copy-start.11 = (f32[32,256]{1,0:T(8,128)}, f32[32,256]{1,0:T(8,128)S(1)}, u32[]{:S(2)}) copy-start(f32[32,256]{1,0:T(8,128)S(1)} %get-tuple-element.263) | copy-start | bytes 98308
  2264.7 270.7 %reduce-scatter.5.cloned.1.call-start = ((), (), s32[]{:S(2)}) async-start(), calls=%async_computation.6 | async-start | bytes 1081344 | tf_op jit(solution)/shard_map/reduce_scatter | solution.py:143
  2402.3 144.5 %copy-start.10 = (f32[256,32]{0,1:T(8,128)S(1)}, f32[256,32]{0,1:T(8,128)}, u32[]{:S(2)}) copy-start(f32[256,32]{0,1:T(8,128)} %reduce-scatter.3.cloned.1.call-done) | copy-start | bytes 98308
  2535.3 9.4 copy-start.12
  2542.1 11.8 all-to-all-start.2
  2554.0 13.3 all-to-all-start.1
  2598.9 32.5 %copy-start.1 = (s32[36864]{0:T(1024)S(1)}, s32[36864]{0:T(1024)}, u32[]{:S(2)}) copy-start(s32[36864]{0:T(1024)} %param.11) | copy-start | bytes 442372
  (1 other events, 0.8 us)
Sparse Core Ops, SparseCore 0:
  2264.8 134.6 reduce-scatter.2
  2401.7 133.5 reduce-scatter.4
where the time goes:
time: 2650 us; the launch traced here: 2640 us
  matrix products  1770 us (67%)
  blocking collectives  389 us (15%)
  waiting for transfers between devices  272 us (10%)
  local copies, waits for them, and re-layouts  113 us (4%)
  other arithmetic  62.7 us (2%)
    dot_general x336, matrix products, low_dot(): return jnp.dot(left, right, preferred_element_type=jnp.float32)  1620 us
    all_gather x1, blocking collectives, local(): ref_strip = lax.all_gather(ref_local, 'grp', axis=1, tiled=True)  379 us
    dot_general x64, matrix products, exact_dot(): jnp.dot(left, right, precision=lax.Precision.HIGHEST, preferred_element_t...  148 us
    reduce_scatter x1, waiting for transfers between devices, local(): lax.psum_scatter(totals[0], ('scan', 'grp'), scatter_dimension=1, tiled=T...  134 us
    reduce_scatter x1, waiting for transfers between devices, local(): lax.psum_scatter(totals[1], ('scan', 'grp'), scatter_dimension=1, tiled=T...  130 us
  transfers between devices with their start and end apart: 5, of which 3 were waited for; matrix products, arithmetic and copies ran while one was open for 2% of the time, Pallas kernels for 0%

commit v1 on v0

v1 whole, which is shorter than its diff:
```python
import functools
import math

import jax
import jax.numpy as jnp
import numpy as np
from jax import lax
from jax.experimental import pallas as pl
from jax.experimental.pallas import tpu as pltpu
from jax.sharding import PartitionSpec as P

LAGS = 16
DEN = 4
REACH = 32
PAD = REACH // DEN
AXES = ("scan", "grp")


def signed(length):
    k = np.arange(length)
    return np.where(k < length // 2, k, k - length)


def tables(product, period):
    angles = 2.0 * np.pi * (product % period) / period
    return jnp.asarray(np.cos(angles), jnp.bfloat16), jnp.asarray(np.sin(angles), jnp.bfloat16)


def low_dot(left, right, dims=((1,), (0,))):
    return lax.dot_general(left, right, (dims, ((), ())), preferred_element_type=jnp.float32)


def split_dot(table, values):
    upper = values.astype(jnp.bfloat16)
    lower = (values - upper.astype(jnp.float32)).astype(jnp.bfloat16)
    return low_dot(table, upper) + low_dot(table, lower)


def shift_add_kernel(shifts, v_ref, acc_ref):
    block, strip_rows, strip_cols = v_ref.shape
    tall, wide = acc_ref.shape[1:]
    step = pl.program_id(0)

    @pl.when(step == 0)
    def _():
        acc_ref[...] = jnp.zeros_like(acc_ref)

    def visit(j, carry):
        p = step * block + j
        sy = shifts[0, p] + REACH
        sx = shifts[1, p] + REACH
        kind = (sx & (DEN - 1)) * DEN + (sy & (DEN - 1))
        v = v_ref[j].astype(jnp.float32)
        v = jnp.concatenate([v, jnp.zeros((strip_rows, wide - strip_cols), jnp.float32)], axis=1)
        v = jnp.concatenate([v, jnp.zeros((tall - strip_rows, wide), jnp.float32)], axis=0)
        acc_ref[kind] += pltpu.roll(pltpu.roll(v, sy >> 2, 0), sx >> 2, 1)
        return carry

    lax.fori_loop(0, block, visit, 0, unroll=2)


def shift_add(shifts, images, tall, wide):
    pixels, strip_rows, strip_cols = images.shape
    block = math.gcd(pixels, 32)
    return pl.pallas_call(
        shift_add_kernel,
        out_shape=jax.ShapeDtypeStruct((DEN * DEN, tall, wide), jnp.float32),
        grid_spec=pltpu.PrefetchScalarGridSpec(
            num_scalar_prefetch=1,
            grid=(pixels // block,),
            in_specs=[pl.BlockSpec((block, strip_rows, strip_cols), lambda i, s: (i, 0, 0))],
            out_specs=pl.BlockSpec((DEN * DEN, tall, wide), lambda i, s: (0, 0, 0)),
        ),
        cost_estimate=pl.CostEstimate(flops=pixels * tall * wide * 8, bytes_accessed=images.size * 2, transcendentals=0),
        name="shift_add",
    )(shifts, images)


def local(frames, dark_frame, gain_frame, bf_index, row_level, shift_num):
    scan_count = lax.axis_size("scan")
    grp_count = lax.axis_size("grp")
    devices = scan_count * grp_count
    strip_rows, strip_cols, pixels = frames.shape
    rows, cols = strip_rows * scan_count, strip_cols * grp_count
    y0 = lax.axis_index("scan") * strip_rows
    x0 = lax.axis_index("grp") * strip_cols
    tall = strip_rows + 2 * PAD
    wide = -(-(strip_cols + 2 * PAD) // 128) * 128
    own_cols = cols // devices

    shifts = lax.all_gather(shift_num, AXES, axis=1, tiled=True)
    dark_pixel = jnp.take(dark_frame, bf_index).astype(jnp.float32) / 256.0
    gain_pixel = jnp.take(gain_frame, bf_index).astype(jnp.float32) / 4096.0
    corrected = (frames.astype(jnp.float32) - row_level[:, None, None] * dark_pixel) * gain_pixel
    ref_local = jnp.sum(corrected, axis=2).astype(jnp.bfloat16)
    strips = corrected.astype(jnp.bfloat16)
    ref_strip = lax.all_gather(ref_local, "grp", axis=1, tiled=True)
    ref_image = lax.all_gather(ref_strip, "scan", axis=0, tiled=True).astype(jnp.float32)

    sums = shift_add(shifts, jnp.transpose(strips, (2, 0, 1)), tall, wide)
    low_sums = sums.astype(jnp.bfloat16).reshape(DEN * DEN * tall, wide)
    kx = np.arange(cols)
    cols_cos, cols_sin = tables(kx[:, None] * np.arange(wide)[None, :], cols)
    zc = low_dot(cols_cos, low_sums, ((1,), (1,))).reshape(cols, DEN, DEN * tall)
    zs = low_dot(cols_sin, low_sums, ((1,), (1,))).reshape(cols, DEN, DEN * tall)
    turn = jnp.mod(
        DEN * jnp.asarray(kx, jnp.int32)[:, None] * (x0 - PAD)
        + jnp.asarray(signed(cols)[:, None] * np.arange(DEN)[None, :], jnp.int32),
        DEN * cols,
    ).astype(jnp.float32) * (2.0 * math.pi / (DEN * cols))
    turn_cos, turn_sin = jnp.cos(turn)[:, :, None], jnp.sin(turn)[:, :, None]
    part_real = jnp.sum(zc * turn_cos - zs * turn_sin, axis=1)
    part_imag = -jnp.sum(zc * turn_sin + zs * turn_cos, axis=1)
    part = jnp.concatenate([part_real, part_imag], axis=1).astype(jnp.bfloat16)

    part = lax.all_to_all(part, AXES, split_axis=0, concat_axis=0, tiled=True)
    part = part.reshape(scan_count, grp_count, own_cols, 2, DEN * tall).astype(jnp.float32)
    part = jnp.sum(part, axis=1).transpose(2, 1, 0, 3).reshape(2, own_cols, scan_count * DEN * tall)
    low_part = part.astype(jnp.bfloat16)
    ky = np.arange(rows)[:, None, None, None]
    place = (
        np.arange(scan_count)[:, None, None] * strip_rows + np.arange(tall)[None, None, :] - PAD
    )[None]
    turn_rows = DEN * ky * place + signed(rows)[:, None, None, None] * np.arange(DEN)[None, None, :, None]
    rows_cos, rows_sin = tables(turn_rows.reshape(rows, scan_count * DEN * tall), DEN * rows)
    last = ((1,), (1,))
    spec_real = low_dot(rows_cos, low_part[0], last) + low_dot(rows_sin, low_part[1], last)
    spec_imag = low_dot(rows_cos, low_part[1], last) - low_dot(rows_sin, low_part[0], last)
    device = lax.axis_index("scan") * grp_count + lax.axis_index("grp")
    anchor = (jnp.arange(rows)[:, None] == 0) & (jnp.arange(own_cols)[None, :] + device * own_cols == 0)
    spec = jnp.concatenate(
        [jnp.where(anchor, 0.0, spec_real), jnp.where(anchor, 0.0, spec_imag)], axis=1
    )
    up_rows_cos, up_rows_sin = tables(np.arange(2 * rows)[:, None] * signed(rows)[None, :], 2 * rows)
    by_cos, by_sin = split_dot(up_rows_cos, spec), split_dot(up_rows_sin, spec)
    column = jnp.concatenate(
        [
            by_cos[:, :own_cols] - by_sin[:, own_cols:],
            by_cos[:, own_cols:] + by_sin[:, :own_cols],
        ],
        axis=1,
    ).astype(jnp.bfloat16)
    column = lax.all_to_all(column, AXES, split_axis=0, concat_axis=0, tiled=True)
    own_rows = 2 * rows // devices
    column = column.reshape(devices, own_rows, 2, own_cols).transpose(2, 1, 0, 3).reshape(2, own_rows, cols)
    up_cols_cos, up_cols_sin = tables(signed(cols)[:, None] * np.arange(2 * cols)[None, :], 2 * cols)
    upsampled = (low_dot(column[0], up_cols_cos) - low_dot(column[1], up_cols_sin)) * (
        1.0 / (rows * cols * math.sqrt(pixels))
    )

    centred = (ref_image - jnp.mean(ref_image)).astype(jnp.bfloat16)
    half = LAGS // 2
    centred = jnp.concatenate([centred[-half:], centred, centred[:half]], axis=0)
    centred = jnp.concatenate([centred[:, -half:], centred, centred[:, :half]], axis=1)
    window = lax.dynamic_slice(centred, (y0, x0), (strip_rows + LAGS, strip_cols + LAGS))
    moved = jnp.stack([window[:, LAGS - b : LAGS - b + strip_cols] for b in range(LAGS)])
    moved = jnp.stack([moved[:, LAGS - a : LAGS - a + strip_rows] for a in range(LAGS)])
    moved = moved.reshape(LAGS * LAGS, strip_rows * strip_cols)
    correl = low_dot(strips.reshape(strip_rows * strip_cols, pixels), moved, ((0,), (1,)))
    correl = (correl * (1.0 / math.sqrt(pixels * rows * cols))).astype(jnp.bfloat16)
    correl = lax.all_to_all(correl, AXES, split_axis=0, concat_axis=0, tiled=True)
    correl = jnp.sum(correl.reshape(devices, pixels // devices, LAGS * LAGS).astype(jnp.float32), axis=0)
    return (upsampled, correl)


def solution(mesh):
    return jax.shard_map(
        local,
        mesh=mesh,
        in_specs=(P("scan", "grp", None), P(), P(), P(), P("scan"), P(None, ("scan", "grp"))),
        out_specs=(P(("scan", "grp"), None), P(("scan", "grp"), None)),
        check_vma=False,
    )
```

time: 2650 us -> 310 us (0.12)
  matrix products: 1770 us -> 18.7 us
  blocking collectives: 389 us -> 106 us
  waiting for transfers between devices: 272 us -> 12.9 us
  Pallas kernels: 0 us -> 61 us
  local copies, waits for them, and re-layouts: 113 us -> 67.9 us
  other arithmetic: 62.7 us -> 29 us
    dot_general x400 -> x13, matrix products: 1770 us -> 18.7 us  [low_dot(): lax.dot_general(left, right, (dims, ((), ())), preferred_element_type=jnp...]
    all_gather x1, blocking collectives: 379 us -> 26.1 us  [local(): ref_strip = lax.all_gather(ref_local, 'grp', axis=1, tiled=True)]
    reduce_scatter x2 -> x0, waiting for transfers between devices: 264 us -> none  [the longest x1 134 us: local(): lax.psum_scatter(totals[0], ('scan', 'grp'), scatter_dimension=1, tiled=T...]
    all_gather x1 -> x2, blocking collectives: 10.3 us -> 80.3 us  [the longest x1 70.3 us: local(): shifts = lax.all_gather(shift_num, AXES, axis=1, tiled=True)]
    pallas_call x0 -> x1, Pallas kernels: none -> 61 us  [shift_add(): pl.pallas_call(shift_add_kernel, out_shape=jax.ShapeDtypeStruct((DEN * DE...]
    sin x64 -> x0, other arithmetic: 43.7 us -> none  [axis_phase(): return (jnp.cos(angles), jnp.sin(angles))]
    reshape x1 -> x2, local copies, waits for them, and re-layouts: 27.4 us -> 0.24 us  [local(): column.reshape(devices, own_rows, 2, own_cols).transpose(2, 1, 0, 3)]
  transfers between devices with their start and end apart: 5 -> 3, of which waited for: 3 -> 2; matrix products, arithmetic and copies ran while one was open for 2% -> 14% of each run, Pallas kernels for 0% -> 0%
where the time goes in v1:
time: 310 us; the launch traced here: 309 us
  blocking collectives  106 us (34%)
  local copies, waits for them, and re-layouts  67.9 us (22%)
  Pallas kernels  61 us (20%)
  other arithmetic  29 us (9%)
  matrix products  18.7 us (6%)
  waiting for transfers between devices  12.9 us (4%)
  starting transfers between devices  11 us (4%)
    all_gather x1, blocking collectives, local(): shifts = lax.all_gather(shift_num, AXES, axis=1, tiled=True)  70.3 us
    pallas_call x1, Pallas kernels, shift_add(): pl.pallas_call(shift_add_kernel, out_shape=jax.ShapeDtypeStruct((DEN * DE...  61 us
    unnamed x60, local copies, waits for them, and re-layouts  50.9 us
    all_gather x1, blocking collectives, local(): ref_strip = lax.all_gather(ref_local, 'grp', axis=1, tiled=True)  26.1 us
    dot_general x13, matrix products, low_dot(): lax.dot_general(left, right, (dims, ((), ())), preferred_element_type=jnp...  18.7 us
    reduce_sum x1, other arithmetic, local(): ref_local = jnp.sum(corrected, axis=2).astype(jnp.bfloat16)  17.6 us
    all_gather x1, blocking collectives, local(): lax.all_gather(ref_strip, 'scan', axis=0, tiled=True).astype(jnp.float32)  10 us
    all_to_all x1, waiting for transfers between devices, local(): lax.all_to_all(correl, AXES, split_axis=0, concat_axis=0, tiled=True)  7.18 us
  transfers between devices with their start and end apart: 3, of which 2 were waited for; matrix products, arithmetic and copies ran while one was open for 14% of the time, Pallas kernels for 0%

profile of v1, /device:TPU:0, one launch (start us, length us, event | category | flops | bytes accessed | tf_op | source)
XLA Modules:
  0.0 308.9 jit_solution(12211490599726948787)
XLA Ops:
  0.7 70.3 %all-gather = s32[32,32,2]{1,2,0:T(2,128)S(1)} all-gather(s32[1,32,2]{1,2,0:T(2,128)} %bitcast.212), channel_id=1, replica_groups=mesh['scan'=8,'grp'=4] {'scan','grp'}, dimensions={0}, use_global_device_ids=true | all-gather | bytes 8448 | tf_op jit(solution)/shard_map/all_gather | solution.py:91
  70.9 0.7 reshape.131
  71.6 24.0 %copy.47 = bf16[32,256,1024]{1,0,2:T(8,128)(2,1)} copy(bf16[32,256,1024]{2,1,0:T(8,128)(2,1)} %param.18) | data formatting | bytes 33554432 | tf_op args[0]
  95.6 6.2 %gather_fusion = s32[1024]{0:T(1024)S(1)} fusion(s32[36864]{0:T(1024)S(1)} %copy-done, s32[1024]{0:T(1024)S(1)} %fusion.39), kind=kCustom, calls=%fused_computation.clone | custom fusion | bytes 12288 | tf_op jit(solution)/shard_map/jit(_take)/gather | solution.py:92
  101.8 6.2 %gather_fusion.1 = s32[1024]{0:T(1024)S(1)} fusion(s32[36864]{0:T(1024)S(1)} %copy-done.2, s32[1024]{0:T(1024)S(1)} %fusion.39), kind=kCustom, calls=%fused_computation.1.clone | custom fusion | bytes 12288 | tf_op jit(solution)/shard_map/jit(_take)/gather | solution.py:93
  108.0 0.2 broadcast_multiply_fusion
  108.2 17.6 %fusion = (bf16[32,256]{1,0:T(8,128)(2,1)S(1)}, bf16[32,256,1024]{1,0,2:T(8,128)(2,1)}) fusion(bf16[32,256,1024]{1,0,2:T(8,128)(2,1)} %copy.47, f32[1024]{0:T(1024)S(1)} %fusion.37, f32[32,1024]{0,1:T(8,128)S(1)} %broadcast_multiply_fusion), kind=kLoop, calls=%fused_computation.3 | loop fusion | flops 41934848 | bytes 33705984 | tf_op jit(solution)/shard_map/reduce_sum | solution.py:95
  125.8 61.0 %shift_add.1 = f32[16,48,384]{2,1,0:T(8,128)} custom-call(s32[2,1024]{1,0:T(2,128)} %bitcast.211, bf16[1024,32,256]{2,1,0:T(8,128)(2,1)} %bitcast.196), custom_call_target="tpu_custom_call" | custom-call | flops 150994944 | bytes 16777216 | tf_op jit(solution)/shard_map/shift_add/pallas_call | solution.py:65
  186.9 1.4 convert_element_type.66
  188.3 2.1 fusion.49
  190.5 2.6 fusion.48
  193.3 3.7 %subtract_reduce_fusion = (bf16[1024,192]{0,1:T(8,128)(2,1)}, f32[1024,192]{0,1:T(8,128)S(1)}) fusion(f32[1024,4,192]{0,2,1:T(8,128)S(1)} %bitcast.198, f32[1024,4,192]{0,2,1:T(8,128)} %bitcast.199, f32[1024,4]{0,1:T(4,128)S(1)} %get-tuple-element.20, f32[1024,4]{0,1:T(4,128)S(1)} %get-tuple-element.19), kind=kLoop, calls=%fused_computation.6 | loop fusion | flops 5898240 | bytes 7503872 | tf_op jit(solution)/shard_map/reduce_sum | solution.py:112
  197.1 0.2 copy.49
  197.3 1.2 copy.48
  198.5 1.2 pad_maximum_fusion
  199.7 2.6 all-to-all-start
  202.3 26.1 %all_gather.10 = bf16[32,1024]{1,0:T(8,128)(2,1)S(1)} all-gather(bf16[32,256]{1,0:T(8,128)(2,1)S(1)} %get-tuple-element.7), channel_id=1, replica_groups=mesh['scan'=8,'grp'=4] {'grp'}, dimensions={1}, use_global_device_ids=true | all-gather | bytes 81920 | tf_op jit(solution)/shard_map/all_gather | solution.py:97
  228.5 10.0 %all_gather.11 = bf16[256,1024]{1,0:T(8,128)(2,1)S(1)} all-gather(bf16[32,1024]{1,0:T(8,128)(2,1)S(1)} %all_gather.10), channel_id=1, replica_groups=mesh['scan'=8,'grp'=4] {'scan'}, dimensions={0}, use_global_device_ids=true | all-gather | bytes 589824 | tf_op jit(solution)/shard_map/all_gather | solution.py:98
  238.5 0.9 convert_reduce_fusion
  240.3 0.7 concatenate.32
  243.7 16.0 %copy.55 = bf16[128,8,32,256]{3,1,2,0:T(8,128)(2,1)S(1)} copy(bf16[128,8,32,256]{3,2,1,0:T(8,128)(2,1)} %bitcast.197) | data formatting | bytes 33554432
  259.7 6.2 %copy.56 = bf16[32,8,32,256]{3,1,2,0:T(8,128)(2,1)} copy(bf16[32,8,32,256]{3,2,1,0:T(8,128)(2,1)S(1)} %bitcast.203) | data formatting | bytes 8388608
  266.0 7.5 %fusion.3 = bf16[1024,256]{1,0:T(8,128)(2,1)} fusion(bf16[8192,1024]{0,1:T(8,128)(2,1)S(1)} %bitcast.200, bf16[256,8192]{1,0:T(8,128)(2,1)} %bitcast.204), kind=kOutput, calls=%fused_computation.12 | convolution fusion | flops 4295491584 | bytes 21495808 | tf_op jit(solution)/shard_map/dot_general | solution.py:30
  273.5 4.2 %all-to-all-start.2 = ((bf16[32,32,256]{2,1,0:T(8,128)(2,1)}), bf16[32,32,256]{2,1,0:T(8,128)(2,1)}, u32[]{:S(2)}, u32[]{:S(2)}) async-start(bf16[32,32,256]{2,1,0:T(8,128)(2,1)} %bitcast.49), calls=%async_computation.2 | async-start | bytes 1048576 | tf_op jit(solution)/shard_map/all_to_all | solution.py:161
  277.7 0.5 convert_element_type.68
  278.3 1.7 reduce
  280.1 0.5 fusion.47
  280.5 0.1 copy.51
  280.7 0.1 squeeze.15
  281.0 0.1 squeeze.14
  281.1 0.3 fusion.51
  281.5 0.3 fusion.50
  281.8 0.3 fusion.7
  282.2 0.3 fusion.9
  282.5 0.2 fusion.33
  282.7 0.2 fusion.35
  282.9 0.2 fusion.4
  283.1 0.2 fusion.5
  283.7 0.8 reshape.136
  284.5 7.2 %all-to-all-done.2 = bf16[32,32,256]{2,1,0:T(8,128)(2,1)} async-done(((bf16[32,32,256]{2,1,0:T(8,128)(2,1)}), bf16[32,32,256]{2,1,0:T(8,128)(2,1)}, u32[]{:S(2)}, u32[]{:S(2)}) %all-to-all-start.2) | async-done | bytes 524320 | tf_op jit(solution)/shard_map/all_to_all | solution.py:161
  291.7 4.2 %all-to-all-start.1 = ((bf16[32,2,512]{2,1,0:T(2,128)(2,1)}), bf16[32,2,512]{2,1,0:T(2,128)(2,1)S(1)}, u32[]{:S(2)}, u32[]{:S(2)}) async-start(bf16[32,2,512]{2,1,0:T(2,128)(2,1)} %reshape.136), calls=%async_computation.1 | async-start | bytes 131072 | tf_op jit(solution)/shard_map/all_to_all | solution.py:143
  295.9 1.7 convert_reduce_fusion.1
  297.6 5.8 %all-to-all-done.1 = bf16[32,2,512]{2,1,0:T(2,128)(2,1)S(1)} async-done(((bf16[32,2,512]{2,1,0:T(2,128)(2,1)}), bf16[32,2,512]{2,1,0:T(2,128)(2,1)S(1)}, u32[]{:S(2)}, u32[]{:S(2)}) %all-to-all-start.1) | async-done | bytes 65568 | tf_op jit(solution)/shard_map/all_to_all | solution.py:143
  303.8 0.2 squeeze.16
  304.0 0.2 squeeze.17
  304.2 3.0 fusion.52
  307.2 0.4 copy-done.3
  307.6 1.3 fusion.2
  (78 shorter events, 4.2 us)
Async XLA Ops:
  0.6 95.0 %copy-start = (s32[36864]{0:T(1024)S(1)}, s32[36864]{0:T(1024)}, u32[]{:S(2)}) copy-start(s32[36864]{0:T(1024)} %param.19) | copy-start | bytes 442372
  71.6 24.0 %copy-start.10 = (s32[1024]{0:T(1024)S(1)}, s32[1024]{0:T(1024)}, u32[]{:S(2)}) copy-start(s32[1024]{0:T(1024)} %param.21) | copy-start | bytes 12292
  95.6 6.2 %copy-start.2 = (s32[36864]{0:T(1024)S(1)}, s32[36864]{0:T(1024)}, u32[]{:S(2)}) copy-start(s32[36864]{0:T(1024)} %param.20) | copy-start | bytes 442372
  95.6 12.4 %copy-start.11 = (f32[32]{0:T(128)S(1)}, f32[32]{0:T(128)}, u32[]{:S(2)}) copy-start(f32[32]{0:T(128)} %param.22) | copy-start | bytes 388
  186.9 3.6 %copy-start.6 = (bf16[1024,384]{1,0:T(8,128)(2,1)S(1)}, bf16[1024,384]{1,0:T(8,128)(2,1)}, u32[]{:S(2)}) copy-start(bf16[1024,384]{1,0:T(8,128)(2,1)} %constant.88.clone) | copy-start | bytes 2359300
  190.5 2.7 copy-start.9
  199.7 73.8 %all-to-all-start = ((bf16[32,32,384]{2,1,0:T(8,128)(2,1)}), bf16[32,32,384]{2,1,0:T(8,128)(2,1)S(1)}, u32[]{:S(2)}, u32[]{:S(2)}) async-start(bf16[32,32,384]{2,1,0:T(8,128)(2,1)} %pad_maximum_fusion), calls=%async_computation | async-start | bytes 1572864 | tf_op jit(solution)/shard_map/all_to_all | solution.py:116
  273.5 7.6 %copy-start.4 = (bf16[256,1536]{1,0:T(8,128)(2,1)S(1)}, bf16[256,1536]{1,0:T(8,128)(2,1)}, u32[]{:S(2)}) copy-start(bf16[256,1536]{1,0:T(8,128)(2,1)} %constant.91.clone) | copy-start | bytes 2359300
  273.5 8.3 %copy-start.5 = (bf16[256,1536]{1,0:T(8,128)(2,1)S(1)}, bf16[256,1536]{1,0:T(8,128)(2,1)}, u32[]{:S(2)}) copy-start(bf16[256,1536]{1,0:T(8,128)(2,1)} %constant.92.clone) | copy-start | bytes 2359300
  273.5 18.2 %all-to-all-start.2 = ((bf16[32,32,256]{2,1,0:T(8,128)(2,1)}), bf16[32,32,256]{2,1,0:T(8,128)(2,1)}, u32[]{:S(2)}, u32[]{:S(2)}) async-start(bf16[32,32,256]{2,1,0:T(8,128)(2,1)} %bitcast.49), calls=%async_computation.2 | async-start | bytes 1048576 | tf_op jit(solution)/shard_map/all_to_all | solution.py:161
  278.3 4.2 %copy-start.8 = (bf16[512,256]{1,0:T(8,128)(2,1)S(1)}, bf16[512,256]{1,0:T(8,128)(2,1)}, u32[]{:S(2)}) copy-start(bf16[512,256]{1,0:T(8,128)(2,1)} %constant.94.clone) | copy-start | bytes 786436
  278.3 4.4 %copy-start.7 = (bf16[512,256]{1,0:T(8,128)(2,1)S(1)}, bf16[512,256]{1,0:T(8,128)(2,1)}, u32[]{:S(2)}) copy-start(bf16[512,256]{1,0:T(8,128)(2,1)} %constant.93.clone) | copy-start | bytes 786436
  291.7 11.7 %all-to-all-start.1 = ((bf16[32,2,512]{2,1,0:T(2,128)(2,1)}), bf16[32,2,512]{2,1,0:T(2,128)(2,1)S(1)}, u32[]{:S(2)}, u32[]{:S(2)}) async-start(bf16[32,2,512]{2,1,0:T(2,128)(2,1)} %reshape.136), calls=%async_computation.1 | async-start | bytes 131072 | tf_op jit(solution)/shard_map/all_to_all | solution.py:143
  304.0 5.0 %copy-start.1 = (s32[36864]{0:T(1024)S(1)}, s32[36864]{0:T(1024)}, u32[]{:S(2)}) copy-start(s32[36864]{0:T(1024)} %param.19) | copy-start | bytes 442372
  304.1 3.5 %copy-start.3 = (bf16[1024,2048]{1,0:T(8,128)(2,1)S(1)}, bf16[1024,2048]{1,0:T(8,128)(2,1)}, u32[]{:S(2)}) copy-start(bf16[1024,2048]{1,0:T(8,128)(2,1)} %constant.96.clone) | copy-start | bytes 12582916
